TPU v7x, 32 devices: a whole 2x2x4 slice. The times are simulated.
32 devices in a mesh: wide: 16 (over z, y, x), narrow: 2 (over core).
Axes of the slice: x: 2, y: 2, z: 4, core: 2. Of those that a mesh axis runs over, the one named last changes fastest.
Arguments:
- contributions: float32 [2, 3, 8192, 128], P('narrow', None, 'wide'), may hold values from -6 to 6
- send_map: int32 [16, 800], P('wide'), may hold values from -1 to 511, as said below
- arrival_map: int32 [16, 800], P('wide'), may hold values from -1 to 255, as said below
- dual_diagonal: float32 [4096, 128], P('wide'), may hold values from 0.5 to 2
- mortar: bfloat16 [4096, 128, 128], P('wide'), may hold values from -0.5 to 0.5
- master_inverse: bfloat16 [4096, 128, 128], P('wide'), may hold values from -0.5 to 0.5
Outputs:
- corrections: float32 [2, 3, 8192, 128], P('narrow', None, 'wide')
Inputs may be any that keep to these rules, and one draw needn't show every extreme that they name: `send_map`: each row 0 to 511 of a partition stands in exactly one of its slots. Some stripe has all 50 of its slots used by every partition. arrival_map[d, o * 50 + c] is -1 exactly where send_map[o, d * 50 + c] is -1.
All inputs are finite; a program needn't handle non-finite values.
Results may differ from a plain program's by a relative error of at most 0.0041.
Values sent between devices are 32-bit elements; how exact they have to be, the bound alone decides.
No kernel may reach another device: no remote copies, remote signals or barrier semaphores. Data moves between devices by JAX's collectives and lax.ppermute only.
A program may use at most 64 MiB of HBM per device.

v0:
```python
import jax
import jax.numpy as jnp
from jax import lax
from jax.sharding import PartitionSpec as P


def partner_2(value, axis, stride):
    mask = 2**stride
    pairs = [(source, source ^ mask) for source in range(lax.axis_size(axis))]
    return lax.ppermute(value, axis, pairs)


def condense(slave_sums, master_sums, diagonal, mortar_part, inverse_part):
    multiplier_low = (slave_sums / diagonal[None]).astype(jnp.bfloat16)
    pushed = jnp.einsum(
        "bij,cbi->cbj", mortar_part, multiplier_low, preferred_element_type=jnp.float32
    )
    condensed_low = (master_sums + pushed).astype(jnp.bfloat16)
    master_fix = jnp.einsum(
        "bkj,cbj->cbk", inverse_part, condensed_low, preferred_element_type=jnp.float32
    )
    master_low = master_fix.astype(jnp.bfloat16)
    slave_fix = (
        jnp.einsum("bij,cbj->cbi", mortar_part, master_low, preferred_element_type=jnp.float32)
        / diagonal[None]
    )
    return (slave_fix, master_fix)


def shards(contributions, send_map, arrival_map, dual_diagonal, mortar, master_inverse):
    my_side = lax.axis_index("narrow")
    block_count = dual_diagonal.shape[0]
    node_count = contributions.shape[3]
    comp_count = contributions.shape[1]
    row_count = contributions.shape[2]
    picked = send_map[0]
    is_live = picked >= 0
    filled = jnp.where(is_live, picked, 0)
    outgoing = jnp.take(contributions[0], filled, axis=1) * is_live[None, :, None].astype(
        jnp.float32
    )
    landing = jnp.where(is_live, picked, row_count)
    block_ids = jnp.arange(block_count, dtype=jnp.int32)
    received_rows = lax.all_to_all(outgoing, "wide", split_axis=1, concat_axis=1, tiled=True)
    choosing_mask = (arrival_map[0][:, None] == block_ids[None, :]).astype(jnp.float32)
    local_row_sums = jnp.einsum(
        "gxp,xt->gtp", received_rows, choosing_mask, precision=lax.Precision.HIGHEST
    )
    partner = partner_2(local_row_sums, "narrow", 0)
    slave_sums = jnp.where(my_side == 0, local_row_sums, partner)
    master_sums = jnp.where(my_side == 0, partner, local_row_sums)
    slave_fix, master_fix = condense(slave_sums, master_sums, dual_diagonal, mortar, master_inverse)
    local_correction = jnp.where(my_side == 0, slave_fix, master_fix)
    departing_rows = jnp.einsum(
        "oxq,ux->ouq", local_correction, choosing_mask, precision=lax.Precision.HIGHEST
    )
    returned = lax.all_to_all(departing_rows, "wide", split_axis=1, concat_axis=1, tiled=True)
    placed = (
        jnp.zeros((comp_count, row_count + 1, node_count), jnp.float32)
        .at[:, landing, :]
        .set(returned)
    )
    return placed[:, :row_count][None]


def solution(mesh):
    placed = (
        P("narrow", None, "wide", None),
        P("wide", None),
        P("wide", None),
        P("wide", None),
        P("wide", None, None),
        P("wide", None, None),
    )
    return jax.shard_map(
        shards,
        mesh=mesh,
        in_specs=placed,
        out_specs=P("narrow", None, "wide", None),
        check_vma=False,
    )
```

profile of v0, /device:TPU:0, one launch (start us, length us, event | category | flops | bytes accessed | tf_op | source)
XLA Modules:
  0.0 153.0 jit_solution(14585886316772614351)
XLA Ops:
  0.0 0.7 fusion.21
  0.7 0.7 reduce.2
  1.5 1.7 %copy.37 = f32[1,3,512,128]{3,1,2,0:T(4,128)S(1)} copy(f32[1,3,512,128]{3,2,1,0:T(8,128)} %param.6) | data formatting | bytes 1572864 | tf_op args[0]
  3.1 3.6 %gather_fusion = f32[800,3,128]{2,1,0:T(4,128)S(1)} fusion(f32[3,512,128]{2,0,1:T(4,128)S(1)} %bitcast.35, s32[1024]{0:T(1024)S(1)} %pad_clamp_fusion), kind=kCustom, calls=%fused_computation | custom fusion | bytes 2460800 | tf_op jit(solution)/shard_map/jit(_take)/gather | solution.py:39
  6.8 5.0 %multiply_bitcast_fusion = f32[3,800,128]{2,0,1:T(4,128)} fusion(f32[800,3,128]{2,1,0:T(4,128)S(1)} %gather_fusion, f32[800]{0:T(1024)S(1)} %get-tuple-element.8, pred[800]{0:T(1024)(128)(4,1)S(1)} %get-tuple-element.7), kind=kLoop, calls=%fused_computation.2 | loop fusion | flops 614400 | bytes 2461600 | tf_op jit(solution)/shard_map/mul | solution.py:39
  11.8 0.0 copy-start.1
  11.8 8.5 %all-to-all-start = ((f32[3,800,128]{2,0,1:T(4,128)}), f32[3,800,128]{2,0,1:T(4,128)S(1)}, u32[]{:S(2)}, u32[]{:S(2)}) async-start(f32[3,800,128]{2,0,1:T(4,128)} %multiply_bitcast_fusion), calls=%async_computation | async-start | bytes 3276800 | tf_op jit(solution)/shard_map/all_to_all | solution.py:44
  20.3 0.0 copy-done.1
  20.3 0.0 copy-start
  20.3 35.2 %all-to-all-done = f32[3,800,128]{2,0,1:T(4,128)S(1)} async-done(((f32[3,800,128]{2,0,1:T(4,128)}), f32[3,800,128]{2,0,1:T(4,128)S(1)}, u32[]{:S(2)}, u32[]{:S(2)}) %all-to-all-start) | async-done | bytes 1228832 | tf_op jit(solution)/shard_map/all_to_all | solution.py:44
  55.5 1.2 fusion.4
  56.7 0.1 collective-permute-start
  56.8 1.7 %collective-permute-done = f32[3,256,128]{2,1,0:T(8,128)S(1)} collective-permute-done((f32[3,256,128]{2,1,0:T(8,128)S(1)}, f32[3,256,128]{2,1,0:T(8,128)S(1)}, u32[]{:S(2)}, u32[]{:S(2)}) %collective-permute-start) | collective-permute-done | bytes 393248 | tf_op jit(solution)/shard_map/ppermute | solution.py:10
  58.5 0.0 copy-done
  58.5 0.1 divide_convert_fusion
  58.5 0.0 slice-start
  58.5 5.8 %fusion.17 = f32[256,3,128]{2,1,0:T(4,128)S(1)} fusion(bf16[256,128,128]{2,1,0:T(8,128)(2,1)} %param.10, bf16[3,256,128]{2,1,0:T(8,128)(2,1)S(1)} %divide_convert_fusion), kind=kOutput, calls=%fused_computation.23 | convolution fusion | flops 25165824 | bytes 8978432 | tf_op jit(solution)/shard_map/bij,cbi->cbj/dot_general | solution.py:15
  64.3 0.0 slice-start.1
  64.3 0.1 fusion.12
  64.4 7.9 %fusion.15 = f32[256,3,128]{2,1,0:T(4,128)S(1)} fusion(bf16[256,128,128]{2,1,0:T(8,128)(2,1)} %param.11, bf16[3,256,128]{2,1,0:T(8,128)(2,1)S(1)} %fusion.12), kind=kOutput, calls=%fused_computation.21 | convolution fusion | flops 25165824 | bytes 8978432 | tf_op jit(solution)/shard_map/bkj,cbj->cbk/dot_general | solution.py:19
  72.4 0.0 slice-done
  72.4 0.0 slice-done.1
  72.4 4.4 %fusion.1 = f32[3,256,128]{2,0,1:T(4,128)S(1)} fusion(f32[256,3,128]{2,1,0:T(4,128)S(1)} %fusion.15, bf16[256,128,128]{2,1,0:T(8,128)(2,1)S(1)} %bitcast.33, f32[256,128]{1,0:T(8,128)S(1)} %copy-done, pred[]{:T(512)S(6)} %eq.24), kind=kOutput, calls=%fused_computation.6 | convolution fusion | flops 25460736 | bytes 9306113 | tf_op jit(solution)/shard_map/bij,cbj->cbi/dot_general | solution.py:24
  76.8 0.9 convolution_bitcast_fusion
  77.7 0.8 copy.23
  78.6 48.1 %all_to_all.10 = f32[3,800,128]{2,0,1:T(4,128)S(1)} all-to-all(f32[3,800,128]{2,0,1:T(4,128)S(1)} %copy.23), channel_id=1, replica_groups=mesh['wide'=16,'narrow'=2] {'wide'}, dimensions={1} | all-to-all | bytes 2457600 | tf_op jit(solution)/shard_map/all_to_all | solution.py:57
  126.6 0.1 broadcast_in_dim.28
  126.8 25.1 %scatter_fusion = f32[3,513,128]{2,0,1:T(4,128)S(1)} fusion(f32[3,513,128]{2,0,1:T(4,128)S(1)} %broadcast_in_dim.28, s32[800]{0:T(1024)S(1)} %get-tuple-element.6, f32[800,3,128]{2,1,0:T(4,128)S(1)} %bitcast.34), kind=kCustom, calls=%fused_computation.1 | custom fusion | bytes 3689600 | tf_op jit(solution)/shard_map/scatter | solution.py:61
  151.9 0.2 slice_bitcast_fusion
  152.1 0.9 copy.24
  (4 shorter events, 0.0 us)
Async XLA Ops:
  11.8 8.5 %copy-start.1 = (s32[1,800]{1,0:T(1,128)S(1)}, s32[1,800]{1,0:T(1,128)}, u32[]{:S(2)}) copy-start(s32[1,800]{1,0:T(1,128)} %param.8) | copy-start | bytes 9604
  11.8 43.7 %all-to-all-start = ((f32[3,800,128]{2,0,1:T(4,128)}), f32[3,800,128]{2,0,1:T(4,128)S(1)}, u32[]{:S(2)}, u32[]{:S(2)}) async-start(f32[3,800,128]{2,0,1:T(4,128)} %multiply_bitcast_fusion), calls=%async_computation | async-start | bytes 3276800 | tf_op jit(solution)/shard_map/all_to_all | solution.py:44
  20.3 38.2 %copy-start = (f32[256,128]{1,0:T(8,128)S(1)}, f32[256,128]{1,0:T(8,128)}, u32[]{:S(2)}) copy-start(f32[256,128]{1,0:T(8,128)} %param.9) | copy-start | bytes 393220
  56.7 1.8 %collective-permute-start = (f32[3,256,128]{2,1,0:T(8,128)S(1)}, f32[3,256,128]{2,1,0:T(8,128)S(1)}, u32[]{:S(2)}, u32[]{:S(2)}) collective-permute-start(f32[3,256,128]{2,1,0:T(8,128)S(1)} %fusion.4), channel_id=1, source_target_pairs={{0,1},{1,0},{2,3},{3,2},{4,5},{5,4},{6,7},{7,6},{8,9},{9,8},{10,11... | collective-permute-start | bytes 1179656 | tf_op jit(solution)/shard_map/ppermute | solution.py:10
  58.5 13.8 %slice-start = ((s8[8388608]{0:T(1024)(128)(4,1)}), s8[4194304]{0:T(1024)(128)(4,1)S(1)}, s32[]{:S(2)}) async-start(s8[8388608]{0:T(1024)(128)(4,1)} %bitcast.32), calls=%async_computation.2 | async-start | bytes 8388608
  64.3 8.0 %slice-start.1 = ((s8[8388608]{0:T(1024)(128)(4,1)}), s8[4194304]{0:T(1024)(128)(4,1)S(1)}, s32[]{:S(2)}) async-start(s8[8388608]{0:T(1024)(128)(4,1)} %bitcast.32), calls=%async_computation.3 | async-start | bytes 8388608
where the time goes:
time: 153 us
  blocking collectives  48.1 us (31%)
  waiting for transfers between devices  36.9 us (24%)
  local copies, waits for them, and re-layouts  32.5 us (21%)
  matrix products  20.3 us (13%)
  starting transfers between devices  8.54 us (6%)
  other arithmetic  6.57 us (4%)
    all_to_all x1, blocking collectives, shards(): lax.all_to_all(departing_rows, 'wide', split_axis=1, concat_axis=1, tiled...  48.1 us
    all_to_all x1, waiting for transfers between devices, shards(): lax.all_to_all(outgoing, 'wide', split_axis=1, concat_axis=1, tiled=True)  35.2 us
    scatter x1, local copies, waits for them, and re-layouts, shards(): placed = jnp.zeros((comp_count, row_count + 1, node_count), jnp.float32)....  25.1 us
    all_to_all x1, starting transfers between devices, shards(): lax.all_to_all(outgoing, 'wide', split_axis=1, concat_axis=1, tiled=True)  8.47 us
    dot_general x1, matrix products, condense(): jnp.einsum('bkj,cbj->cbk', inverse_part, condensed_low, preferred_element...  7.93 us
    dot_general x1, matrix products, condense(): jnp.einsum('bij,cbi->cbj', mortar_part, multiplier_low, preferred_element...  5.8 us
    mul x1, other arithmetic, shards(): jnp.take(contributions[0], filled, axis=1)  4.99 us
    dot_general x1, matrix products, condense(): jnp.einsum('bij,cbj->cbi', mortar_part, master_low, preferred_element_typ...  4.45 us
  transfers between devices with their start and end apart: 2, of which 2 were waited for; matrix products, arithmetic and copies ran while one was open for 0% of the time, Pallas kernels for 0%

commit v1 on v0

--- a/solution.py
+++ b/solution.py
@@ -54,7 +54,16 @@
     departing_rows = jnp.einsum(
         "oxq,ux->ouq", local_correction, choosing_mask, precision=lax.Precision.HIGHEST
     )
-    returned = lax.all_to_all(departing_rows, "wide", split_axis=1, concat_axis=1, tiled=True)
+    _bind_heaps = lambda row_data, dim_k, dimension_no: jnp.concatenate(
+        jax.lax.all_to_all(
+            jnp.stack(jnp.split(row_data, jax.lax.axis_size("wide"), axis=dim_k)),
+            axis_name="wide",
+            split_axis=0,
+            concat_axis=0,
+        ),
+        axis=dimension_no,
+    )
+    returned = _bind_heaps(departing_rows, 1, dimension_no=1)
     placed = (
         jnp.zeros((comp_count, row_count + 1, node_count), jnp.float32)
         .at[:, landing, :]

time: 153 us -> 147 us (0.961)
  blocking collectives: 48.1 us -> 41.9 us
    all_to_all x1, blocking collectives: 48.1 us -> 41.9 us  [shards(): jax.lax.all_to_all(jnp.stack(jnp.split(row_data, jax.lax.axis_size('wide'...]
where the time goes in v1:
time: 147 us; the launch traced here: 146 us
  blocking collectives  41.9 us (29%)
  waiting for transfers between devices  36.9 us (25%)
  local copies, waits for them, and re-layouts  32.5 us (22%)
  matrix products  20.3 us (14%)
  starting transfers between devices  8.54 us (6%)
  other arithmetic  5.95 us (4%)
    all_to_all x1, blocking collectives, shards(): jax.lax.all_to_all(jnp.stack(jnp.split(row_data, jax.lax.axis_size('wide'...  41.9 us
    all_to_all x1, waiting for transfers between devices, shards(): lax.all_to_all(outgoing, 'wide', split_axis=1, concat_axis=1, tiled=True)  35.2 us
    scatter x1, local copies, waits for them, and re-layouts, shards(): placed = jnp.zeros((comp_count, row_count + 1, node_count), jnp.float32)....  24.8 us
    all_to_all x1, starting transfers between devices, shards(): lax.all_to_all(outgoing, 'wide', split_axis=1, concat_axis=1, tiled=True)  8.47 us
    dot_general x1, matrix products, condense(): jnp.einsum('bkj,cbj->cbk', inverse_part, condensed_low, preferred_element...  7.93 us
    dot_general x1, matrix products, condense(): jnp.einsum('bij,cbi->cbj', mortar_part, multiplier_low, preferred_element...  5.8 us
    mul x1, other arithmetic, shards(): jnp.take(contributions[0], filled, axis=1)  4.99 us
    dot_general x1, matrix products, condense(): jnp.einsum('bij,cbj->cbi', mortar_part, master_low, preferred_element_typ...  4.45 us
  transfers between devices with their start and end apart: 2, of which 2 were waited for; matrix products, arithmetic and copies ran while one was open for 0% of the time, Pallas kernels for 0%

profile of v1, /device:TPU:0, one launch (start us, length us, event | category | flops | bytes accessed | tf_op | source)
XLA Modules:
  0.0 146.4 jit_solution(4216280213869555110)
XLA Ops:
  0.0 0.0 copy-start.1
  0.0 0.8 fusion.37
  0.8 1.7 %copy.38 = f32[1,3,512,128]{3,1,2,0:T(4,128)S(1)} copy(f32[1,3,512,128]{3,2,1,0:T(8,128)} %param.6) | data formatting | bytes 1572864 | tf_op args[0]
  2.5 0.0 copy-done.1
  2.5 3.6 %gather_fusion = f32[800,3,128]{2,1,0:T(4,128)S(1)} fusion(f32[3,512,128]{2,0,1:T(4,128)S(1)} %bitcast.99, s32[1024]{0:T(1024)S(1)} %pad_clamp_fusion), kind=kCustom, calls=%fused_computation | custom fusion | bytes 2460800 | tf_op jit(solution)/shard_map/jit(_take)/gather | solution.py:39
  6.2 5.0 %multiply_bitcast_fusion = f32[3,800,128]{2,0,1:T(4,128)} fusion(f32[800,3,128]{2,1,0:T(4,128)S(1)} %gather_fusion, f32[800]{0:T(1024)S(1)} %get-tuple-element.8, pred[800]{0:T(1024)(128)(4,1)S(1)} %get-tuple-element.7), kind=kLoop, calls=%fused_computation.2 | loop fusion | flops 614400 | bytes 2461600 | tf_op jit(solution)/shard_map/mul | solution.py:39
  11.2 0.0 copy-start.2
  11.2 8.5 %all-to-all-start = ((f32[3,800,128]{2,0,1:T(4,128)}), f32[3,800,128]{2,0,1:T(4,128)S(1)}, u32[]{:S(2)}, u32[]{:S(2)}) async-start(f32[3,800,128]{2,0,1:T(4,128)} %multiply_bitcast_fusion), calls=%async_computation | async-start | bytes 3276800 | tf_op jit(solution)/shard_map/all_to_all | solution.py:44
  19.7 0.0 copy-done.2
  19.7 0.0 copy-start
  19.7 35.2 %all-to-all-done = f32[3,800,128]{2,0,1:T(4,128)S(1)} async-done(((f32[3,800,128]{2,0,1:T(4,128)}), f32[3,800,128]{2,0,1:T(4,128)S(1)}, u32[]{:S(2)}, u32[]{:S(2)}) %all-to-all-start) | async-done | bytes 1228832 | tf_op jit(solution)/shard_map/all_to_all | solution.py:44
  54.9 1.2 fusion.4
  56.1 0.1 collective-permute-start
  56.2 1.7 %collective-permute-done = f32[3,256,128]{2,1,0:T(8,128)S(1)} collective-permute-done((f32[3,256,128]{2,1,0:T(8,128)S(1)}, f32[3,256,128]{2,1,0:T(8,128)S(1)}, u32[]{:S(2)}, u32[]{:S(2)}) %collective-permute-start) | collective-permute-done | bytes 393248 | tf_op jit(solution)/shard_map/ppermute | solution.py:10
  57.9 0.0 copy-done
  57.9 0.1 divide_convert_fusion
  57.9 0.0 slice-start
  57.9 5.8 %fusion.17 = f32[256,3,128]{2,1,0:T(4,128)S(1)} fusion(bf16[256,128,128]{2,1,0:T(8,128)(2,1)} %param.10, bf16[3,256,128]{2,1,0:T(8,128)(2,1)S(1)} %divide_convert_fusion), kind=kOutput, calls=%fused_computation.23 | convolution fusion | flops 25165824 | bytes 8978432 | tf_op jit(solution)/shard_map/bij,cbi->cbj/dot_general | solution.py:15
  63.7 0.0 slice-start.1
  63.7 0.1 fusion.12
  63.8 7.9 %fusion.15 = f32[256,3,128]{2,1,0:T(4,128)S(1)} fusion(bf16[256,128,128]{2,1,0:T(8,128)(2,1)} %param.11, bf16[3,256,128]{2,1,0:T(8,128)(2,1)S(1)} %fusion.12), kind=kOutput, calls=%fused_computation.21 | convolution fusion | flops 25165824 | bytes 8978432 | tf_op jit(solution)/shard_map/bkj,cbj->cbk/dot_general | solution.py:19
  71.8 0.0 slice-done
  71.8 0.0 slice-done.1
  71.8 4.4 %fusion.1 = f32[3,256,128]{2,0,1:T(4,128)S(1)} fusion(f32[256,3,128]{2,1,0:T(4,128)S(1)} %fusion.15, bf16[256,128,128]{2,1,0:T(8,128)(2,1)S(1)} %bitcast.97, f32[256,128]{1,0:T(8,128)S(1)} %copy-done, pred[]{:T(512)S(6)} %eq.24), kind=kOutput, calls=%fused_computation.6 | convolution fusion | flops 25460736 | bytes 9306113 | tf_op jit(solution)/shard_map/bij,cbj->cbi/dot_general | solution.py:24
  76.2 0.9 convolution_bitcast_fusion
  77.4 41.9 %all_to_all.10 = f32[16,3,50,128]{3,2,1,0:T(8,128)S(1)} all-to-all(f32[16,3,50,128]{3,2,1,0:T(8,128)S(1)} %fusion.20), channel_id=1, replica_groups=mesh['wide'=16,'narrow'=2] {'wide'}, dimensions={0} | all-to-all | bytes 2457600 | tf_op jit(solution)/shard_map/all_to_all | solution.py:58
  119.3 0.1 copy.23
  119.4 0.1 reshape.82
  119.5 0.8 copy.24
  120.4 0.1 broadcast_in_dim.28
  120.5 24.8 %scatter_fusion = f32[3,513,128]{2,0,1:T(4,128)S(1)} fusion(f32[3,513,128]{2,0,1:T(4,128)S(1)} %broadcast_in_dim.28, s32[800]{0:T(1024)S(1)} %get-tuple-element.6, f32[800,3,128]{2,1,0:T(4,128)S(1)} %copy.24), kind=kCustom, calls=%fused_computation.1 | custom fusion | bytes 3689600 | tf_op jit(solution)/shard_map/scatter | solution.py:70
  145.3 0.2 slice_bitcast_fusion
  145.5 0.9 copy.25
  (21 shorter events, 0.2 us)
Async XLA Ops:
  0.0 2.5 %copy-start.1 = (s32[1,800]{1,0:T(1,128)S(1)}, s32[1,800]{1,0:T(1,128)}, u32[]{:S(2)}) copy-start(s32[1,800]{1,0:T(1,128)} %param.7) | copy-start | bytes 9604
  11.2 8.5 %copy-start.2 = (s32[1,800]{1,0:T(1,128)S(1)}, s32[1,800]{1,0:T(1,128)}, u32[]{:S(2)}) copy-start(s32[1,800]{1,0:T(1,128)} %param.8) | copy-start | bytes 9604
  11.2 43.7 %all-to-all-start = ((f32[3,800,128]{2,0,1:T(4,128)}), f32[3,800,128]{2,0,1:T(4,128)S(1)}, u32[]{:S(2)}, u32[]{:S(2)}) async-start(f32[3,800,128]{2,0,1:T(4,128)} %multiply_bitcast_fusion), calls=%async_computation | async-start | bytes 3276800 | tf_op jit(solution)/shard_map/all_to_all | solution.py:44
  19.7 38.2 %copy-start = (f32[256,128]{1,0:T(8,128)S(1)}, f32[256,128]{1,0:T(8,128)}, u32[]{:S(2)}) copy-start(f32[256,128]{1,0:T(8,128)} %param.9) | copy-start | bytes 393220
  56.1 1.8 %collective-permute-start = (f32[3,256,128]{2,1,0:T(8,128)S(1)}, f32[3,256,128]{2,1,0:T(8,128)S(1)}, u32[]{:S(2)}, u32[]{:S(2)}) collective-permute-start(f32[3,256,128]{2,1,0:T(8,128)S(1)} %fusion.4), channel_id=1, source_target_pairs={{0,1},{1,0},{2,3},{3,2},{4,5},{5,4},{6,7},{7,6},{8,9},{9,8},{10,11... | collective-permute-start | bytes 1179656 | tf_op jit(solution)/shard_map/ppermute | solution.py:10
  57.9 13.8 %slice-start = ((s8[8388608]{0:T(1024)(128)(4,1)}), s8[4194304]{0:T(1024)(128)(4,1)S(1)}, s32[]{:S(2)}) async-start(s8[8388608]{0:T(1024)(128)(4,1)} %bitcast.96), calls=%async_computation.2 | async-start | bytes 8388608
  63.7 8.0 %slice-start.1 = ((s8[8388608]{0:T(1024)(128)(4,1)}), s8[4194304]{0:T(1024)(128)(4,1)S(1)}, s32[]{:S(2)}) async-start(s8[8388608]{0:T(1024)(128)(4,1)} %bitcast.96), calls=%async_computation.3 | async-start | bytes 8388608
